TPU v7x, 32 devices: a whole 2x2x4 slice. The times are simulated.
32 devices in a mesh: rep: 4 (over y, x), fsdp: 4 (over z), tp: 2 (over core).
Axes of the slice: x: 2, y: 2, z: 4, core: 2. Of those that a mesh axis runs over, the one named last changes fastest.
Arguments:
- hidden: bfloat16 [4096, 4096], P(('rep', 'fsdp')), may hold values from -6 to 6
- norm_gain: float32 [4096], P('fsdp'), may hold values from 0.5 to 1.5
- value_weight: bfloat16 [4096, 1024], P('fsdp', 'tp'), may hold values from -0.09375 to 0.09375
- value_grad: bfloat16 [4096, 1024], P(('rep', 'fsdp'), 'tp'), may hold values from -6 to 6
Outputs:
- input_grad: bfloat16 [4096, 4096], P(('rep', 'fsdp'))
- weight_grad: float32 [4096, 1024], P('fsdp', 'tp')
- gain_grad: float32 [4096], P('fsdp')
All inputs are finite; a program needn't handle non-finite values.
Results may differ from a plain program's by a relative error of at most 0.00125.
Values may be sent and summed in bfloat16 or wider, within the bound.
A program may use at most 64 MiB of HBM per device.

v0:
```python
import jax
import jax.numpy as jnp
from jax import lax
from jax.sharding import PartitionSpec as P

D = 4096
epsilon = 1e-05


def shards(hidden, norm_gain, value_weight, value_grad):
    average = 1.0 / (lax.axis_size("rep") * lax.axis_size("fsdp"))
    inputs = hidden.astype(jnp.float32)
    inv_local = lax.rsqrt(jnp.mean(inputs * inputs, axis=1, keepdims=True) + epsilon)
    columns = lax.all_to_all(hidden, "fsdp", split_axis=1, concat_axis=0, tiled=True)
    inv_rms = lax.all_gather(inv_local, "fsdp", axis=0, tiled=True)
    normal = columns.astype(jnp.float32) * inv_rms
    normed = (normal * norm_gain).astype(jnp.bfloat16)
    group_grad = lax.all_gather(value_grad, "fsdp", axis=0, tiled=True)
    partial_grad = jnp.dot(group_grad, value_weight.T, preferred_element_type=jnp.float32)
    grad_normed = lax.psum(partial_grad, "tp")
    weight_part = jnp.dot(normed.T, group_grad, preferred_element_type=jnp.float32)
    gain_part = jnp.sum(grad_normed * normal, axis=0)
    grad_scaled = grad_normed * norm_gain
    row_total = lax.psum(
        jnp.sum(grad_scaled * normal, axis=1, keepdims=True).astype(jnp.bfloat16), "fsdp"
    ).astype(jnp.float32)
    center = row_total / D
    column_grad = (inv_rms * (grad_scaled - normal * center)).astype(jnp.bfloat16)
    input_grad = lax.all_to_all(column_grad, "fsdp", split_axis=0, concat_axis=1, tiled=True)
    weight_total = lax.psum(weight_part, "rep")
    gain_total = lax.psum(gain_part, "rep")
    return (input_grad, weight_total * average, gain_total * average)


def solution(mesh):
    placed = (P(("rep", "fsdp"), None), P("fsdp"), P("fsdp", "tp"), P(("rep", "fsdp"), "tp"))
    return jax.shard_map(
        shards,
        mesh=mesh,
        in_specs=placed,
        out_specs=(P(("rep", "fsdp"), None), P("fsdp", "tp"), P("fsdp")),
        check_vma=False,
    )
```

profile of v0, /device:TPU:0, one launch (start us, length us, event | category | flops | bytes accessed | tf_op | source)
XLA Modules:
  0.0 209.7 jit_solution(1176009656137438168)
XLA Ops:
  7.2 0.0 copy-start
  7.2 0.0 all-gather.4.cloned.1.call-start
  7.2 0.7 all-gather.4.cloned.1.call-update
  7.9 0.0 all-reduce.3.cloned.1.call-start
  8.0 32.3 %all-gather.4.cloned.1.call-done = bf16[1024,512]{1,0:T(8,128)(2,1)} async-done(((bf16[256,512]{1,0:T(8,128)(2,1)}), bf16[1024,512]{1,0:T(8,128)(2,1)}) %all-gather.4.cloned.1.call-update) | async-done | bytes 1048592 | tf_op jit(solution)/shard_map/all_gather | solution.py:18
  40.3 0.0 copy-done
  40.3 4.5 %fusion = f32[1024,1024]{1,0:T(8,128)} fusion(bf16[1024,512]{1,0:T(8,128)(2,1)} %all-gather.4.cloned.1.call-done, bf16[1024,512]{1,0:T(8,128)(2,1)S(1)} %copy-done), kind=kOutput, calls=%fused_computation.11 | convolution fusion | flops 1073741824 | bytes 6291456 | tf_op jit(solution)/shard_map/dot_general | solution.py:19
  44.8 0.0 copy-start.1
  44.8 0.0 all-reduce.3.cloned.1.call-update
  44.8 1.6 copy-done.1
  46.4 1.5 copy.16
  47.9 0.0 copy-start.2
  47.9 3.8 %all-to-all-start = ((bf16[256,4,1024]{2,0,1:T(8,128)(2,1)}), bf16[256,4,1024]{2,0,1:T(8,128)(2,1)S(1)}, u32[]{:S(2)}, u32[]{:S(2)}) async-start(bf16[256,4,1024]{2,0,1:T(8,128)(2,1)} %bitcast.29), calls=%async_computation | async-start | bytes 4194304 | tf_op jit(solution)/shard_map/all_to_all | solution.py:14
  51.7 2.6 %multiply_reduce_fusion.2 = f32[256]{0:T(256)S(1)} fusion(bf16[256,4096]{1,0:T(8,128)(2,1)} %param.4), kind=kLoop, calls=%fused_computation.5 | loop fusion | flops 3145472 | bytes 2098176 | tf_op jit(solution)/shard_map/reduce_sum | solution.py:13
  54.4 36.9 %all-gather.1 = f32[4,1,256]{2,1,0:T(1,128)S(1)} all-gather(f32[1,1,256]{2,1,0:T(1,128)S(1)} %bitcast.35), channel_id=2, replica_groups=mesh['rep'=4,'fsdp'=4,'tp'=2] {'fsdp'}, dimensions={0}, use_global_device_ids=true | all-gather | bytes 5120 | tf_op jit(solution)/shard_map/all_gather | solution.py:15
  91.3 8.4 %all-to-all-done = bf16[256,4,1024]{2,0,1:T(8,128)(2,1)S(1)} async-done(((bf16[256,4,1024]{2,0,1:T(8,128)(2,1)}), bf16[256,4,1024]{2,0,1:T(8,128)(2,1)S(1)}, u32[]{:S(2)}, u32[]{:S(2)}) %all-to-all-start) | async-done | bytes 2097184 | tf_op jit(solution)/shard_map/all_to_all | solution.py:14
  99.7 0.0 all-reduce.3.cloned.1.call-done
  99.7 0.0 copy-done.2
  99.7 3.3 %multiply_reduce_fusion = (f32[1024]{0:T(1024)S(1)}, bf16[1024]{0:T(1024)(128)(2,1)S(1)}) fusion(f32[1024,1024]{1,0:T(8,128)} %all-reduce.3.cloned.1.call-done, bf16[256,4,1024]{2,0,1:T(8,128)(2,1)S(1)} %all-to-all-done, f32[1024]{0:T(1024)S(1)} %bitcast.32, f32[1024]{0:T(1024)S(1)} %copy-done.2), kind=kLoop, calls=%fused_computation.1 | loop fusion | flops 7337984 | bytes 6305792 | tf_op jit(solution)/shard_map/reduce_sum | solution.py:22
  103.0 11.9 %psum.29 = bf16[1024,1]{0,1:T(2,128)(2,1)S(1)} all-reduce(bf16[1024,1]{0,1:T(2,128)(2,1)S(1)} %convert_element_type.40), channel_id=1, replica_groups=mesh['rep'=4,'fsdp'=4,'tp'=2] {'fsdp'}, use_global_device_ids=true, to_apply=%region_3.0 | all-reduce | flops 1024 | bytes 4096 | tf_op jit(solution)/shard_map/psum | solution.py:24
  115.0 4.3 %multiply_convert_fusion = (bf16[1024,1024]{1,0:T(8,128)(2,1)}, bf16[1024,1024]{1,0:T(8,128)(2,1)}) fusion(bf16[256,4,1024]{2,0,1:T(8,128)(2,1)S(1)} %all-to-all-done, f32[1024]{0:T(1024)S(1)} %bitcast.33, f32[1024]{0:T(1024)S(1)} %copy-done.2, f32[1024]{0:T(1024)S(1)} %bitcast.34, f32[1024,1024]{1,0:T(8,128)} %all-reduce.3.cloned.1.call-done), kind=kLoop, calls=%fused_computation.2 | loop fusion | flops 9437184 | bytes 10498048 | tf_op jit(solution)/shard_map/convert_element_type | solution.py:17
  119.3 3.6 %all-to-all-start.1 = ((bf16[4,256,1024]{2,1,0:T(8,128)(2,1)}), bf16[4,256,1024]{2,1,0:T(8,128)(2,1)S(1)}, u32[]{:S(2)}, u32[]{:S(2)}) async-start(bf16[4,256,1024]{2,1,0:T(8,128)(2,1)} %bitcast.30), calls=%async_computation.1 | async-start | bytes 4194304 | tf_op jit(solution)/shard_map/all_to_all | solution.py:29
  122.9 0.0 all-reduce.5.cloned.1.call-start
  122.9 4.5 %fusion.1 = f32[1024,512]{1,0:T(8,128)} fusion(bf16[1024,1024]{1,0:T(8,128)(2,1)} %get-tuple-element.5, bf16[1024,512]{1,0:T(8,128)(2,1)} %all-gather.4.cloned.1.call-done), kind=kOutput, calls=%fused_computation.12 | convolution fusion | flops 1073741824 | bytes 5242880 | tf_op jit(solution)/shard_map/dot_general | solution.py:21
  127.4 0.0 all-reduce.5.cloned.1.call-update
  127.4 10.0 %psum.31 = f32[1024]{0:T(1024)S(1)} all-reduce(f32[1024]{0:T(1024)S(1)} %get-tuple-element.3), channel_id=1, replica_groups=mesh['rep'=4,'fsdp'=4,'tp'=2] {'rep'}, use_global_device_ids=true, to_apply=%region_6.0 | all-reduce | flops 1024 | bytes 8192 | tf_op jit(solution)/shard_map/psum | solution.py:31
  137.4 0.6 broadcast_multiply_fusion.1
  138.0 60.4 %all-reduce.5.cloned.1.call-done = f32[1024,512]{1,0:T(8,128)} async-done(((f32[1024,512]{1,0:T(8,128)}), f32[1024,512]{1,0:T(8,128)}) %all-reduce.5.cloned.1.call-update) | async-done | bytes 2097168 | tf_op jit(solution)/shard_map/psum | solution.py:30
  198.4 3.1 %broadcast_multiply_fusion = f32[1024,512]{1,0:T(8,128)} fusion(f32[1024,512]{1,0:T(8,128)} %all-reduce.5.cloned.1.call-done), kind=kLoop, calls=%fused_computation.7 | loop fusion | flops 524288 | bytes 4194304 | tf_op jit(solution)/shard_map/mul | solution.py:32
  201.6 0.0 all-to-all-done.1
  201.6 1.6 copy.14
  (3 shorter events, 0.0 us)
Async XLA Ops:
  7.2 33.1 %copy-start = (bf16[1024,512]{1,0:T(8,128)(2,1)S(1)}, bf16[1024,512]{1,0:T(8,128)(2,1)}, u32[]{:S(2)}) copy-start(bf16[1024,512]{1,0:T(8,128)(2,1)} %param.6) | copy-start | bytes 3145732
  7.2 33.1 %all-gather.4.cloned.1.call-start = ((), (), s32[]{:S(2)}) async-start(), calls=%async_computation.2 | async-start | bytes 1310720 | tf_op jit(solution)/shard_map/all_gather | solution.py:18
  7.9 91.8 %all-reduce.3.cloned.1.call-start = ((), (), s32[]{:S(2)}) async-start(), calls=%async_computation.3 | async-start | bytes 8388608 | tf_op jit(solution)/shard_map/psum | solution.py:20
  44.8 1.6 copy-start.1
  47.9 51.8 %copy-start.2 = (f32[1024]{0:T(1024)S(1)}, f32[1024]{0:T(1024)}, u32[]{:S(2)}) copy-start(f32[1024]{0:T(1024)} %param.5) | copy-start | bytes 12292
  47.9 51.8 %all-to-all-start = ((bf16[256,4,1024]{2,0,1:T(8,128)(2,1)}), bf16[256,4,1024]{2,0,1:T(8,128)(2,1)S(1)}, u32[]{:S(2)}, u32[]{:S(2)}) async-start(bf16[256,4,1024]{2,0,1:T(8,128)(2,1)} %bitcast.29), calls=%async_computation | async-start | bytes 4194304 | tf_op jit(solution)/shard_map/all_to_all | solution.py:14
  119.3 82.3 %all-to-all-start.1 = ((bf16[4,256,1024]{2,1,0:T(8,128)(2,1)}), bf16[4,256,1024]{2,1,0:T(8,128)(2,1)S(1)}, u32[]{:S(2)}, u32[]{:S(2)}) async-start(bf16[4,256,1024]{2,1,0:T(8,128)(2,1)} %bitcast.30), calls=%async_computation.1 | async-start | bytes 4194304 | tf_op jit(solution)/shard_map/all_to_all | solution.py:29
  122.9 75.6 %all-reduce.5.cloned.1.call-start = ((), (), s32[]{:S(2)}) async-start(), calls=%async_computation.4 | async-start | bytes 4194304 | tf_op jit(solution)/shard_map/psum | solution.py:30
Sparse Core Ops, SparseCore 0:
  9.6 30.6 all-gather.3
  44.9 27.4 all-reduce.2
  127.6 70.8 all-reduce.4
where the time goes:
time: 210 us
  waiting for transfers between devices  102 us (49%)
  blocking collectives  58.8 us (28%)
  other arithmetic  14 us (7%)
  between operations  13.8 us (7%)
  matrix products  8.97 us (4%)
  starting transfers between devices  7.52 us (4%)
  local copies, waits for them, and re-layouts  4.69 us (2%)
    psum x1, waiting for transfers between devices, shards(): weight_total = lax.psum(weight_part, 'rep')  60.4 us
    all_gather x1, blocking collectives, shards(): inv_rms = lax.all_gather(inv_local, 'fsdp', axis=0, tiled=True)  36.9 us
    all_gather x1, waiting for transfers between devices, shards(): group_grad = lax.all_gather(value_grad, 'fsdp', axis=0, tiled=True)  32.3 us
    psum x1, blocking collectives, shards(): lax.psum(jnp.sum(grad_scaled * normal, axis=1, keepdims=True).astype(jnp....  11.9 us
    psum x1, blocking collectives, shards(): gain_total = lax.psum(gain_part, 'rep')  9.96 us
    all_to_all x1, waiting for transfers between devices, shards(): lax.all_to_all(hidden, 'fsdp', split_axis=1, concat_axis=0, tiled=True)  8.42 us
    dot_general x1, matrix products, shards(): jnp.dot(normed.T, group_grad, preferred_element_type=jnp.float32)  4.49 us
    dot_general x1, matrix products, shards(): jnp.dot(group_grad, value_weight.T, preferred_element_type=jnp.float32)  4.47 us
  transfers between devices with their start and end apart: 5, of which 3 were waited for; matrix products, arithmetic and copies ran while one was open for 6% of the time, Pallas kernels for 0%

commit v1 on v0

--- a/solution.py
+++ b/solution.py
@@ -11,7 +11,10 @@
     average = 1.0 / (lax.axis_size("rep") * lax.axis_size("fsdp"))
     inputs = hidden.astype(jnp.float32)
     inv_local = lax.rsqrt(jnp.mean(inputs * inputs, axis=1, keepdims=True) + epsilon)
-    columns = lax.all_to_all(hidden, "fsdp", split_axis=1, concat_axis=0, tiled=True)
+    columns = jnp.concatenate(
+        lax.all_to_all(jnp.stack(jnp.split(hidden, lax.axis_size("fsdp"), axis=1)), "fsdp", 0, 0),
+        axis=0,
+    )
     inv_rms = lax.all_gather(inv_local, "fsdp", axis=0, tiled=True)
     normal = columns.astype(jnp.float32) * inv_rms
     normed = (normal * norm_gain).astype(jnp.bfloat16)

time: 210 us -> 222 us (1.057)
  waiting for transfers between devices: 102 us -> 113 us
    psum x1, waiting for transfers between devices: 60.4 us -> 71.3 us  [shards(): weight_total = lax.psum(weight_part, 'rep')]
  transfers between devices with their start and end apart: 5 -> 5, of which waited for: 3 -> 3; matrix products, arithmetic and copies ran while one was open for 6% -> 5% of each run, Pallas kernels for 0% -> 0%
where the time goes in v1:
time: 222 us
  waiting for transfers between devices  113 us (51%)
  blocking collectives  57.7 us (26%)
  other arithmetic  15.8 us (7%)
  between operations  13.8 us (6%)
  matrix products  8.43 us (4%)
  starting transfers between devices  8.21 us (4%)
  local copies, waits for them, and re-layouts  4.91 us (2%)
    psum x1, waiting for transfers between devices, shards(): weight_total = lax.psum(weight_part, 'rep')  71.3 us
    all_gather x1, blocking collectives, shards(): inv_rms = lax.all_gather(inv_local, 'fsdp', axis=0, tiled=True)  36.8 us
    all_gather x1, waiting for transfers between devices, shards(): group_grad = lax.all_gather(value_grad, 'fsdp', axis=0, tiled=True)  32.3 us
    psum x1, blocking collectives, shards(): lax.psum(jnp.sum(grad_scaled * normal, axis=1, keepdims=True).astype(jnp....  11.9 us
    psum x1, blocking collectives, shards(): gain_total = lax.psum(gain_part, 'rep')  8.9 us
    all_to_all x1, waiting for transfers between devices, shards(): lax.all_to_all(jnp.stack(jnp.split(hidden, lax.axis_size('fsdp'), axis=1)...  8.42 us
    dot_general x1, matrix products, shards(): jnp.dot(group_grad, value_weight.T, preferred_element_type=jnp.float32)  4.47 us
    convert_element_type x1, other arithmetic, shards(): (inv_rms * (grad_scaled - normal * center)).astype(jnp.bfloat16)  4.45 us
  transfers between devices with their start and end apart: 5, of which 3 were waited for; matrix products, arithmetic and copies ran while one was open for 5% of the time, Pallas kernels for 0%

profile of v1, /device:TPU:0, one launch (start us, length us, event | category | flops | bytes accessed | tf_op | source)
XLA Modules:
  0.0 221.6 jit_solution(16710363575894698421)
XLA Ops:
  7.2 0.0 copy-start
  7.2 0.0 all-gather.4.cloned.1.call-start
  7.2 0.7 all-gather.4.cloned.1.call-update
  7.9 0.0 all-reduce.3.cloned.1.call-start
  8.0 32.3 %all-gather.4.cloned.1.call-done = bf16[1024,512]{1,0:T(8,128)(2,1)} async-done(((bf16[256,512]{1,0:T(8,128)(2,1)}), bf16[1024,512]{1,0:T(8,128)(2,1)}) %all-gather.4.cloned.1.call-update) | async-done | bytes 1048592 | tf_op jit(solution)/shard_map/all_gather | solution.py:21
  40.3 0.0 copy-done
  40.3 4.5 %fusion.14 = f32[1024,1024]{1,0:T(8,128)} fusion(bf16[1024,512]{1,0:T(8,128)(2,1)} %all-gather.4.cloned.1.call-done, bf16[1024,512]{1,0:T(8,128)(2,1)S(1)} %copy-done), kind=kOutput, calls=%fused_computation.24 | convolution fusion | flops 1073741824 | bytes 6291456 | tf_op jit(solution)/shard_map/dot_general | solution.py:22
  44.8 0.0 copy-start.1
  44.8 0.0 all-reduce.3.cloned.1.call-update
  44.8 1.6 copy-done.1
  46.4 0.2 slice_bitcast_fusion.3
  46.5 1.6 pad_maximum_fusion
  48.1 3.7 %all-to-all-start = ((bf16[4,256,1024]{2,1,0:T(8,128)(2,1)}), bf16[4,256,1024]{2,1,0:T(8,128)(2,1)S(1)}, u32[]{:S(2)}, u32[]{:S(2)}) async-start(bf16[4,256,1024]{2,1,0:T(8,128)(2,1)} %pad_maximum_fusion), calls=%async_computation | async-start | bytes 4194304 | tf_op jit(solution)/shard_map/all_to_all | solution.py:15
  51.8 0.0 copy-start.2
  51.8 2.7 %multiply_reduce_fusion = f32[256]{0:T(256)S(1)} fusion(bf16[256,4096]{1,0:T(8,128)(2,1)} %param.4), kind=kLoop, calls=%fused_computation.11 | loop fusion | flops 3145472 | bytes 2098176 | tf_op jit(solution)/shard_map/reduce_sum | solution.py:13
  54.5 36.8 %all-gather.1 = f32[4,1,256]{2,1,0:T(1,128)S(1)} all-gather(f32[1,1,256]{2,1,0:T(1,128)S(1)} %bitcast.30), channel_id=2, replica_groups=mesh['rep'=4,'fsdp'=4,'tp'=2] {'fsdp'}, dimensions={0}, use_global_device_ids=true | all-gather | bytes 5120 | tf_op jit(solution)/shard_map/all_gather | solution.py:18
  91.4 8.4 %all-to-all-done = bf16[4,256,1024]{2,1,0:T(8,128)(2,1)S(1)} async-done(((bf16[4,256,1024]{2,1,0:T(8,128)(2,1)}), bf16[4,256,1024]{2,1,0:T(8,128)(2,1)S(1)}, u32[]{:S(2)}, u32[]{:S(2)}) %all-to-all-start) | async-done | bytes 2097184 | tf_op jit(solution)/shard_map/all_to_all | solution.py:15
  99.8 0.0 all-reduce.3.cloned.1.call-done
  99.8 0.0 copy-done.2
  99.8 3.3 %fusion.9 = (f32[1024]{0:T(1024)S(1)}, bf16[1024]{0:T(1024)(128)(2,1)S(1)}) fusion(f32[1024,1024]{1,0:T(8,128)} %all-reduce.3.cloned.1.call-done, bf16[4,256,1024]{2,1,0:T(8,128)(2,1)S(1)} %all-to-all-done, f32[1024]{0:T(1024)S(1)} %bitcast.26, f32[1024]{0:T(1024)S(1)} %copy-done.2), kind=kLoop, calls=%fused_computation.10 | loop fusion | flops 7337984 | bytes 6305792 | tf_op jit(solution)/shard_map/reduce_sum | solution.py:25
  103.1 11.9 %psum.29 = bf16[1024,1]{0,1:T(2,128)(2,1)S(1)} all-reduce(bf16[1024,1]{0,1:T(2,128)(2,1)S(1)} %convert_element_type.36), channel_id=1, replica_groups=mesh['rep'=4,'fsdp'=4,'tp'=2] {'fsdp'}, use_global_device_ids=true, to_apply=%region_3.0 | all-reduce | flops 1024 | bytes 4096 | tf_op jit(solution)/shard_map/psum | solution.py:27
  115.1 4.4 %fusion.7 = bf16[1024,1024]{1,0:T(8,128)(2,1)} fusion(f32[1024,1024]{1,0:T(8,128)} %all-reduce.3.cloned.1.call-done, bf16[4,256,1024]{2,1,0:T(8,128)(2,1)S(1)} %all-to-all-done, f32[1024]{0:T(1024)S(1)} %bitcast.27, f32[1024]{0:T(1024)S(1)} %bitcast.29, f32[1024]{0:T(1024)S(1)} %copy-done.2), kind=kLoop, calls=%fused_computation.8 | loop fusion | flops 7340032 | bytes 8400896 | tf_op jit(solution)/shard_map/convert_element_type | solution.py:31
  119.5 4.4 %all-to-all-start.1 = ((bf16[4,256,1024]{2,1,0:T(8,128)(2,1)}), bf16[4,256,1024]{2,1,0:T(8,128)(2,1)}, u32[]{:S(2)}, u32[]{:S(2)}) async-start(bf16[4,256,1024]{2,1,0:T(8,128)(2,1)} %bitcast.24), calls=%async_computation.1 | async-start | bytes 4194304 | tf_op jit(solution)/shard_map/all_to_all | solution.py:32
  124.0 0.0 all-reduce.5.cloned.1.call-start
  124.0 4.0 %fusion.10 = f32[1024,512]{1,0:T(8,128)} fusion(bf16[1024,512]{1,0:T(8,128)(2,1)} %all-gather.4.cloned.1.call-done, bf16[1024,1024]{1,0:T(8,128)(2,1)S(1)} %bitcast.23, f32[1024]{0:T(1024)S(1)} %bitcast.28, f32[1024]{0:T(1024)S(1)} %copy-done.2), kind=kOutput, calls=%fused_computation.12 | convolution fusion | flops 1077936128 | bytes 5251072 | tf_op jit(solution)/shard_map/dot_general | solution.py:24
  128.0 0.0 all-reduce.5.cloned.1.call-update
  128.0 71.3 %all-reduce.5.cloned.1.call-done = f32[1024,512]{1,0:T(8,128)} async-done(((f32[1024,512]{1,0:T(8,128)}), f32[1024,512]{1,0:T(8,128)}) %all-reduce.5.cloned.1.call-update) | async-done | bytes 2097168 | tf_op jit(solution)/shard_map/psum | solution.py:33
  199.3 3.1 %broadcast_multiply_fusion = f32[1024,512]{1,0:T(8,128)} fusion(f32[1024,512]{1,0:T(8,128)} %all-reduce.5.cloned.1.call-done), kind=kLoop, calls=%fused_computation.16 | loop fusion | flops 524288 | bytes 4194304 | tf_op jit(solution)/shard_map/mul | solution.py:35
  202.5 8.9 %psum.31 = f32[1024]{0:T(1024)S(1)} all-reduce(f32[1024]{0:T(1024)S(1)} %get-tuple-element.3), channel_id=1, replica_groups=mesh['rep'=4,'fsdp'=4,'tp'=2] {'rep'}, use_global_device_ids=true, to_apply=%region_6.0 | all-reduce | flops 1024 | bytes 8192 | tf_op jit(solution)/shard_map/psum | solution.py:34
  211.4 0.6 broadcast_multiply_fusion.1
  212.0 0.0 all-to-all-done.1
  212.0 3.2 %copy.10 = bf16[4,32,8,1024]{3,2,0,1:T(8,128)(2,1)} copy(bf16[4,32,8,1024]{3,2,1,0:T(8,128)(2,1)} %bitcast.11) | data formatting | bytes 4194304 | tf_op jit(solution)/shard_map/all_to_all | solution.py:32
  (3 shorter events, 0.0 us)
Async XLA Ops:
  7.2 33.1 %copy-start = (bf16[1024,512]{1,0:T(8,128)(2,1)S(1)}, bf16[1024,512]{1,0:T(8,128)(2,1)}, u32[]{:S(2)}) copy-start(bf16[1024,512]{1,0:T(8,128)(2,1)} %param.6) | copy-start | bytes 3145732
  7.2 33.1 %all-gather.4.cloned.1.call-start = ((), (), s32[]{:S(2)}) async-start(), calls=%async_computation.2 | async-start | bytes 1310720 | tf_op jit(solution)/shard_map/all_gather | solution.py:21
  7.9 91.9 %all-reduce.3.cloned.1.call-start = ((), (), s32[]{:S(2)}) async-start(), calls=%async_computation.3 | async-start | bytes 8388608 | tf_op jit(solution)/shard_map/psum | solution.py:23
  44.8 1.6 copy-start.1
  48.1 51.7 %all-to-all-start = ((bf16[4,256,1024]{2,1,0:T(8,128)(2,1)}), bf16[4,256,1024]{2,1,0:T(8,128)(2,1)S(1)}, u32[]{:S(2)}, u32[]{:S(2)}) async-start(bf16[4,256,1024]{2,1,0:T(8,128)(2,1)} %pad_maximum_fusion), calls=%async_computation | async-start | bytes 4194304 | tf_op jit(solution)/shard_map/all_to_all | solution.py:15
  51.8 48.0 %copy-start.2 = (f32[1024]{0:T(1024)S(1)}, f32[1024]{0:T(1024)}, u32[]{:S(2)}) copy-start(f32[1024]{0:T(1024)} %param.5) | copy-start | bytes 12292
  119.5 92.4 %all-to-all-start.1 = ((bf16[4,256,1024]{2,1,0:T(8,128)(2,1)}), bf16[4,256,1024]{2,1,0:T(8,128)(2,1)}, u32[]{:S(2)}, u32[]{:S(2)}) async-start(bf16[4,256,1024]{2,1,0:T(8,128)(2,1)} %bitcast.24), calls=%async_computation.1 | async-start | bytes 4194304 | tf_op jit(solution)/shard_map/all_to_all | solution.py:32
  124.0 75.3 %all-reduce.5.cloned.1.call-start = ((), (), s32[]{:S(2)}) async-start(), calls=%async_computation.4 | async-start | bytes 4194304 | tf_op jit(solution)/shard_map/psum | solution.py:33
Sparse Core Ops, SparseCore 0:
  9.6 30.6 all-gather.3
  44.9 27.4 all-reduce.2
  128.5 70.7 all-reduce.4
